TPU v7x, 32 devices: a whole 2x2x4 slice. The times are simulated.
32 devices in a mesh: tok: 2 (over x), vocab: 16 (over z, y, core).
Axes of the slice: x: 2, y: 2, z: 4, core: 2. Of those that a mesh axis runs over, the one named last changes fastest.
Arguments:
- hidden: bfloat16 [1536, 4096], P('tok', 'vocab'), as said below
- weight: bfloat16 [4096, 16384], P('tok', 'vocab'), may hold values from -0.09375 to 0.09375
- targets: int32 [1536], P('tok'), may hold values from 0 to 16383
- domains: int32 [1536], P('tok'), may hold values from 0 to 63
- seq_len: int32 [12], P('tok'), may hold values from 1 to 128
Outputs:
- token_loss: float32 [1536], P(('tok', 'vocab'))
- domain_mean: float32 [64], replicated
Inputs may be any that keep to these rules, and one draw needn't show every extreme that they name: hidden states of the eval window.
All inputs are finite; a program needn't handle non-finite values.
Results may differ from a plain program's by a relative error of at most 0.0003.
Values may be sent and summed in bfloat16 or wider, within the bound.
A program may use at most 64 MiB of HBM per device.

v0:
```python
import jax
import jax.numpy as jnp
from jax import lax
from jax.sharding import PartitionSpec as P

SEQ_LEN = 128
DOMAINS = 64


def body(hidden, weight, targets, domains, seq_len):
    features = lax.all_gather(hidden, "vocab", axis=1, tiled=True)
    tok_rows = features.shape[0]
    columns = weight.shape[1]
    logits = jnp.dot(
        features,
        lax.all_gather(weight, "tok", axis=0, tiled=True),
        preferred_element_type=jnp.float32,
    )
    first_col = lax.axis_index("vocab") * columns
    column_ids = first_col + lax.broadcasted_iota(jnp.int32, (tok_rows, columns), 1)
    picked_loc = jnp.sum(jnp.where(column_ids == targets[:, None], logits, 0.0), axis=1)
    top_loc = jnp.max(logits, axis=1)
    groups = lax.axis_size("vocab")
    share_len = tok_rows // groups
    share_start = lax.axis_index("vocab") * share_len
    sum_loc = jnp.sum(jnp.exp(logits - top_loc[:, None]), axis=1)
    gathered = (
        lax.all_to_all(
            top_loc.reshape(groups, share_len), "vocab", split_axis=0, concat_axis=0, tiled=True
        ),
        lax.all_to_all(
            sum_loc.reshape(groups, share_len), "vocab", split_axis=0, concat_axis=0, tiled=True
        ),
        lax.all_to_all(
            picked_loc.reshape(groups, share_len), "vocab", split_axis=0, concat_axis=0, tiled=True
        ),
    )
    row_top = jnp.max(gathered[0], axis=0)
    row_total = jnp.sum(gathered[1] * jnp.exp(gathered[0] - row_top[None, :]), axis=0)
    picked = jnp.sum(gathered[2], axis=0)
    loss_raw = jnp.log(row_total) + row_top - picked
    positions = share_start + lax.iota(jnp.int32, share_len)
    seq_ids = positions // SEQ_LEN
    seq_count = seq_len.shape[0]
    lengths = jnp.sum(
        jnp.where(
            seq_ids[:, None] == lax.broadcasted_iota(jnp.int32, (share_len, seq_count), 1),
            seq_len[None, :],
            0,
        ),
        axis=1,
    )
    valid_mask = (positions % SEQ_LEN < lengths).astype(jnp.float32)
    token_loss = loss_raw * valid_mask
    domain_share = lax.dynamic_slice_in_dim(domains, share_start, share_len)
    onehot = (
        domain_share[:, None] == lax.broadcasted_iota(jnp.int32, (share_len, DOMAINS), 1)
    ).astype(jnp.float32)
    domain_sum = jnp.dot(token_loss, onehot, precision=lax.Precision.HIGHEST)
    domain_count = jnp.dot(valid_mask, onehot, precision=lax.Precision.HIGHEST)
    domain_sum, domain_count = lax.psum((domain_sum, domain_count), ("tok", "vocab"))
    domain_mean = domain_sum / jnp.maximum(domain_count, 1.0)
    return (token_loss, domain_mean)


def solution(mesh):
    in_specs = (P("tok", "vocab"), P("tok", "vocab"), P("tok"), P("tok"), P("tok"))
    out_specs = (P(("tok", "vocab")), P())
    return jax.shard_map(body, mesh=mesh, in_specs=in_specs, out_specs=out_specs, check_vma=False)
```

profile of v0, /device:TPU:0, one launch (start us, length us, event | category | flops | bytes accessed | tf_op | source)
XLA Modules:
  0.0 270.7 jit_solution(16608660790201364310)
XLA Ops:
  7.2 0.0 all-gather.5.cloned.1.call-start
  7.2 0.7 all-gather.5.cloned.1.call-update
  7.9 0.0 all-gather.3.cloned.1.call-start
  7.9 0.7 all-gather.3.cloned.1.call-update
  8.7 0.0 copy-start
  8.7 107.6 %all-gather.5.cloned.1.call-done = bf16[4096,1024]{1,0:T(8,128)(2,1)} async-done(((bf16[2048,1024]{1,0:T(8,128)(2,1)}), bf16[4096,1024]{1,0:T(8,128)(2,1)}) %all-gather.5.cloned.1.call-update) | async-done | bytes 8388624 | tf_op jit(solution)/shard_map/all_gather | solution.py:16
  116.2 67.4 %all-gather.3.cloned.1.call-done = bf16[768,4096]{1,0:T(8,128)(2,1)} async-done(((bf16[768,256]{1,0:T(8,128)(2,1)}), bf16[768,4096]{1,0:T(8,128)(2,1)}) %all-gather.3.cloned.1.call-update) | async-done | bytes 6291472 | tf_op jit(solution)/shard_map/all_gather | solution.py:11
  183.7 11.1 %fusion.6 = (f32[768]{0:T(1024)S(1)}, f32[768,1024]{1,0:T(8,128)S(1)}) fusion(bf16[768,4096]{1,0:T(8,128)(2,1)} %all-gather.3.cloned.1.call-done, bf16[4096,1024]{1,0:T(8,128)(2,1)} %all-gather.5.cloned.1.call-done), kind=kOutput, calls=%fused_computation.22 | convolution fusion | flops 6443236352 | bytes 17828864 | tf_op jit(solution)/shard_map/dot_general | solution.py:14
  194.8 0.0 copy-start.2
  194.8 0.7 all_to_all.25
  195.4 3.4 %all-to-all-start.1 = ((f32[16,1,48]{2,1,0:T(1,128)}), f32[16,1,48]{2,1,0:T(1,128)S(1)}, u32[]{:S(2)}, u32[]{:S(2)}) async-start(f32[16,1,48]{2,1,0:T(1,128)} %all_to_all.25), calls=%async_computation.1 | async-start | bytes 16384 | tf_op jit(solution)/shard_map/all_to_all | solution.py:28
  198.9 0.0 copy-done
  198.9 0.9 exponential_reduce_fusion
  199.8 0.7 all_to_all.28
  200.5 4.8 %all-to-all-done.1 = f32[16,1,48]{2,1,0:T(1,128)S(1)} async-done(((f32[16,1,48]{2,1,0:T(1,128)}), f32[16,1,48]{2,1,0:T(1,128)S(1)}, u32[]{:S(2)}, u32[]{:S(2)}) %all-to-all-start.1) | async-done | bytes 3104 | tf_op jit(solution)/shard_map/all_to_all | solution.py:28
  205.3 3.5 %all-to-all-start.2 = ((f32[16,1,48]{2,1,0:T(1,128)}), f32[16,1,48]{2,1,0:T(1,128)S(1)}, u32[]{:S(2)}, u32[]{:S(2)}) async-start(f32[16,1,48]{2,1,0:T(1,128)} %all_to_all.28), calls=%async_computation.2 | async-start | bytes 16384 | tf_op jit(solution)/shard_map/all_to_all | solution.py:34
  208.8 0.0 copy-done.2
  208.8 0.1 select_reduce_fusion.1
  208.9 0.8 dynamic_slice.3
  209.6 0.7 all_to_all.22
  210.3 4.9 %all-to-all-done.2 = f32[16,1,48]{2,1,0:T(1,128)S(1)} async-done(((f32[16,1,48]{2,1,0:T(1,128)}), f32[16,1,48]{2,1,0:T(1,128)S(1)}, u32[]{:S(2)}, u32[]{:S(2)}) %all-to-all-start.2) | async-done | bytes 3104 | tf_op jit(solution)/shard_map/all_to_all | solution.py:34
  215.2 3.4 %all-to-all-start = ((f32[16,1,48]{2,1,0:T(1,128)}), f32[16,1,48]{2,1,0:T(1,128)S(1)}, u32[]{:S(2)}, u32[]{:S(2)}) async-start(f32[16,1,48]{2,1,0:T(1,128)} %all_to_all.22), calls=%async_computation | async-start | bytes 16384 | tf_op jit(solution)/shard_map/all_to_all | solution.py:31
  218.6 0.2 convolution_bitcast_fusion
  218.8 6.1 %all-to-all-done = f32[16,1,48]{2,1,0:T(1,128)S(1)} async-done(((f32[16,1,48]{2,1,0:T(1,128)}), f32[16,1,48]{2,1,0:T(1,128)S(1)}, u32[]{:S(2)}, u32[]{:S(2)}) %all-to-all-start) | async-done | bytes 3104 | tf_op jit(solution)/shard_map/all_to_all | solution.py:31
  225.0 0.0 copy-start.1
  225.0 0.2 convolution_bitcast_fusion.1
  225.2 38.2 %all-reduce = (f32[64]{0:T(128)S(1)}, f32[64]{0:T(128)S(1)}) all-reduce(f32[64]{0:T(128)S(1)} %convolution_bitcast_fusion.1, f32[64]{0:T(128)S(1)} %convolution_bitcast_fusion), channel_id=1, replica_groups=mesh['tok'=2,'vocab'=16] {'tok','vocab'}, use_global_device_ids=true, to_apply=%region_7.8 | all-reduce | flops 128 | bytes 1024 | tf_op jit(solution)/shard_map/psum | solution.py:61
  263.4 0.5 maximum_divide_fusion
  263.9 0.0 copy-done.1
  (6 shorter events, 0.1 us)
Async XLA Ops:
  7.2 109.1 %all-gather.5.cloned.1.call-start = ((), (), s32[]{:S(2)}) async-start(), calls=%async_computation.4 | async-start | bytes 12582912 | tf_op jit(solution)/shard_map/all_gather | solution.py:16
  7.9 175.8 %all-gather.3.cloned.1.call-start = ((), (), s32[]{:S(2)}) async-start(), calls=%async_computation.3 | async-start | bytes 6684672 | tf_op jit(solution)/shard_map/all_gather | solution.py:11
  8.7 190.2 %copy-start = (s32[768]{0:T(1024)S(1)}, s32[768]{0:T(1024)}, u32[]{:S(2)}) copy-start(s32[768]{0:T(1024)} %param.7) | copy-start | bytes 9220
  194.8 14.0 %copy-start.2 = (s32[6]{0:T(128)S(1)}, s32[6]{0:T(128)}, u32[]{:S(2)}) copy-start(s32[6]{0:T(128)} %param.9) | copy-start | bytes 76
  195.4 9.8 %all-to-all-start.1 = ((f32[16,1,48]{2,1,0:T(1,128)}), f32[16,1,48]{2,1,0:T(1,128)S(1)}, u32[]{:S(2)}, u32[]{:S(2)}) async-start(f32[16,1,48]{2,1,0:T(1,128)} %all_to_all.25), calls=%async_computation.1 | async-start | bytes 16384 | tf_op jit(solution)/shard_map/all_to_all | solution.py:28
  205.3 9.9 %all-to-all-start.2 = ((f32[16,1,48]{2,1,0:T(1,128)}), f32[16,1,48]{2,1,0:T(1,128)S(1)}, u32[]{:S(2)}, u32[]{:S(2)}) async-start(f32[16,1,48]{2,1,0:T(1,128)} %all_to_all.28), calls=%async_computation.2 | async-start | bytes 16384 | tf_op jit(solution)/shard_map/all_to_all | solution.py:34
  215.2 9.8 %all-to-all-start = ((f32[16,1,48]{2,1,0:T(1,128)}), f32[16,1,48]{2,1,0:T(1,128)S(1)}, u32[]{:S(2)}, u32[]{:S(2)}) async-start(f32[16,1,48]{2,1,0:T(1,128)} %all_to_all.22), calls=%async_computation | async-start | bytes 16384 | tf_op jit(solution)/shard_map/all_to_all | solution.py:31
  225.0 38.9 %copy-start.1 = (f32[48]{0:T(128)}, f32[48]{0:T(128)S(1)}, u32[]{:S(2)}) copy-start(f32[48]{0:T(128)S(1)} %subtract_select_fusion) | copy-start | bytes 580
Sparse Core Ops, SparseCore 0:
  9.5 106.6 all-gather.4
  118.4 65.2 all-gather.2
where the time goes:
time: 271 us
  waiting for transfers between devices  192 us (71%)
  blocking collectives  38.2 us (14%)
  between operations  14.1 us (5%)
  matrix products  11.4 us (4%)
  starting transfers between devices  10.4 us (4%)
  local copies, waits for them, and re-layouts  2.8 us (1%)
    all_gather x1, waiting for transfers between devices, body(): lax.all_gather(weight, 'tok', axis=0, tiled=True)  108 us
    all_gather x1, waiting for transfers between devices, body(): features = lax.all_gather(hidden, 'vocab', axis=1, tiled=True)  67.4 us
    psum x1, blocking collectives, body(): lax.psum((domain_sum, domain_count), ('tok', 'vocab'))  38.2 us
    dot_general x1, matrix products, body(): jnp.dot(features, lax.all_gather(weight, 'tok', axis=0, tiled=True), pref...  11.1 us
    all_to_all x1, waiting for transfers between devices, body(): lax.all_to_all(sum_loc.reshape(groups, share_len), 'vocab', split_axis=0,...  6.14 us
  transfers between devices with their start and end apart: 5, of which 5 were waited for; matrix products, arithmetic and copies ran while one was open for 1% of the time, Pallas kernels for 0%

commit v1 on v0

--- a/solution.py
+++ b/solution.py
@@ -13,7 +13,11 @@
     columns = weight.shape[1]
     logits = jnp.dot(
         features,
-        lax.all_gather(weight, "tok", axis=0, tiled=True),
+        jnp.roll(
+            jnp.concatenate([weight, lax.ppermute(weight, "tok", [(0, 1), (1, 0)])], axis=0),
+            lax.axis_index("tok") * weight.shape[0],
+            axis=0,
+        ),
         preferred_element_type=jnp.float32,
     )
     first_col = lax.axis_index("vocab") * columns

time: 271 us -> 199 us (0.73)
  waiting for transfers between devices: 192 us -> 108 us
  matrix products: 11.4 us -> 18.3 us
  starting transfers between devices: 10.4 us -> 16.2 us
    all_gather x1 -> x0, waiting for transfers between devices: 108 us -> none  [body(): lax.all_gather(weight, 'tok', axis=0, tiled=True)]
    ppermute x0 -> x1, waiting for transfers between devices: none -> 90.8 us  [body(): lax.ppermute(weight, 'tok', [(0, 1), (1, 0)])]
    all_gather x1, waiting for transfers between devices: 67.4 us -> 0.01 us  [body(): features = lax.all_gather(hidden, 'vocab', axis=1, tiled=True)]
    dot_general x1, matrix products: 11.1 us -> 17.9 us  [body(): jnp.dot(features, jnp.roll(jnp.concatenate([weight, lax.ppermute(weight,...]
    ppermute x0 -> x1, starting transfers between devices: none -> 3.03 us  [body(): lax.ppermute(weight, 'tok', [(0, 1), (1, 0)])]
    all_to_all x1, starting transfers between devices: 3.41 us -> 6.18 us  [body(): lax.all_to_all(top_loc.reshape(groups, share_len), 'vocab', split_axis=0,...]
  transfers between devices with their start and end apart: 5 -> 5, of which waited for: 5 -> 4; matrix products, arithmetic and copies ran while one was open for 1% -> 1% of each run, Pallas kernels for 0% -> 0%
where the time goes in v1:
time: 199 us; the launch traced here: 198 us
  waiting for transfers between devices  108 us (54%)
  blocking collectives  38.2 us (19%)
  matrix products  18.3 us (9%)
  starting transfers between devices  16.2 us (8%)
  between operations  14.1 us (7%)
  local copies, waits for them, and re-layouts  2.8 us (1%)
    ppermute x1, waiting for transfers between devices, body(): lax.ppermute(weight, 'tok', [(0, 1), (1, 0)])  90.8 us
    psum x1, blocking collectives, body(): lax.psum((domain_sum, domain_count), ('tok', 'vocab'))  38.2 us
    dot_general x1, matrix products, body(): jnp.dot(features, jnp.roll(jnp.concatenate([weight, lax.ppermute(weight,...  17.9 us
    all_to_all x1, starting transfers between devices, body(): lax.all_to_all(top_loc.reshape(groups, share_len), 'vocab', split_axis=0,...  6.18 us
    all_to_all x1, waiting for transfers between devices, body(): lax.all_to_all(sum_loc.reshape(groups, share_len), 'vocab', split_axis=0,...  6.14 us
    all_to_all x1, waiting for transfers between devices, body(): lax.all_to_all(top_loc.reshape(groups, share_len), 'vocab', split_axis=0,...  4.99 us
    all_to_all x1, waiting for transfers between devices, body(): lax.all_to_all(picked_loc.reshape(groups, share_len), 'vocab', split_axis...  4.87 us
  transfers between devices with their start and end apart: 5, of which 4 were waited for; matrix products, arithmetic and copies ran while one was open for 1% of the time, Pallas kernels for 0%

profile of v1, /device:TPU:0, one launch (start us, length us, event | category | flops | bytes accessed | tf_op | source)
XLA Modules:
  0.0 198.5 jit_solution(5273640786038862610)
XLA Ops:
  7.2 0.0 all-gather.2.cloned.1.call-start
  7.2 0.7 all-gather.2.cloned.1.call-update
  7.9 3.0 %collective-permute-start = (bf16[2048,1024]{1,0:T(8,128)(2,1)}, bf16[2048,1024]{1,0:T(8,128)(2,1)}, u32[]{:S(2)}, u32[]{:S(2)}) collective-permute-start(bf16[2048,1024]{1,0:T(8,128)(2,1)} %param.6), channel_id=1, source_target_pairs={{0,16},{16,0},{1,17},{17,1},{2,18},{18,2},{3,19},{19,3},{4,20},{20... | collective-permute-start | bytes 12582920 | tf_op jit(solution)/shard_map/ppermute | solution.py:17
  11.0 0.0 copy-start
  11.0 0.0 copy-start.2
  11.0 90.8 %collective-permute-done = bf16[2048,1024]{1,0:T(8,128)(2,1)} collective-permute-done((bf16[2048,1024]{1,0:T(8,128)(2,1)}, bf16[2048,1024]{1,0:T(8,128)(2,1)}, u32[]{:S(2)}, u32[]{:S(2)}) %collective-permute-start) | collective-permute-done | bytes 4194336 | tf_op jit(solution)/shard_map/ppermute | solution.py:17
  101.8 0.0 all-gather.2.cloned.1.call-done
  101.8 17.9 %fusion.16 = (f32[768]{0:T(1024)S(1)}, f32[1024,768]{1,0:T(8,128)S(1)}) fusion(bf16[768,4096]{1,0:T(8,128)(2,1)} %all-gather.2.cloned.1.call-done, s32[]{:T(128)S(6)} %select_n.43, bf16[2048,1024]{1,0:T(8,128)(2,1)} %param.6, bf16[2048,1024]{1,0:T(8,128)(2,1)} %collective-permute-done), kind=kOutput, calls=%fused_computation.35 | convolution fusion | flops 6476790784 | bytes 17828868 | tf_op jit(solution)/shard_map/dot_general | solution.py:14
  119.7 0.7 all_to_all.25
  120.4 6.2 %all-to-all-start.1 = ((f32[16,1,48]{2,1,0:T(1,128)}), f32[16,1,48]{2,1,0:T(1,128)S(1)}, u32[]{:S(2)}, u32[]{:S(2)}) async-start(f32[16,1,48]{2,1,0:T(1,128)} %all_to_all.25), calls=%async_computation.1 | async-start | bytes 16384 | tf_op jit(solution)/shard_map/all_to_all | solution.py:32
  126.6 0.0 copy-done
  126.6 0.7 fusion.6
  127.3 0.7 all_to_all.28
  128.0 5.0 %all-to-all-done.1 = f32[16,1,48]{2,1,0:T(1,128)S(1)} async-done(((f32[16,1,48]{2,1,0:T(1,128)}), f32[16,1,48]{2,1,0:T(1,128)S(1)}, u32[]{:S(2)}, u32[]{:S(2)}) %all-to-all-start.1) | async-done | bytes 3104 | tf_op jit(solution)/shard_map/all_to_all | solution.py:32
  133.0 3.5 %all-to-all-start.2 = ((f32[16,1,48]{2,1,0:T(1,128)}), f32[16,1,48]{2,1,0:T(1,128)S(1)}, u32[]{:S(2)}, u32[]{:S(2)}) async-start(f32[16,1,48]{2,1,0:T(1,128)} %all_to_all.28), calls=%async_computation.2 | async-start | bytes 16384 | tf_op jit(solution)/shard_map/all_to_all | solution.py:38
  136.5 0.0 copy-done.2
  136.5 0.1 select_reduce_fusion
  136.6 0.8 dynamic_slice.8
  137.4 0.7 all_to_all.22
  138.0 4.9 %all-to-all-done.2 = f32[16,1,48]{2,1,0:T(1,128)S(1)} async-done(((f32[16,1,48]{2,1,0:T(1,128)}), f32[16,1,48]{2,1,0:T(1,128)S(1)}, u32[]{:S(2)}, u32[]{:S(2)}) %all-to-all-start.2) | async-done | bytes 3104 | tf_op jit(solution)/shard_map/all_to_all | solution.py:38
  142.9 3.4 %all-to-all-start = ((f32[16,1,48]{2,1,0:T(1,128)}), f32[16,1,48]{2,1,0:T(1,128)S(1)}, u32[]{:S(2)}, u32[]{:S(2)}) async-start(f32[16,1,48]{2,1,0:T(1,128)} %all_to_all.22), calls=%async_computation | async-start | bytes 16384 | tf_op jit(solution)/shard_map/all_to_all | solution.py:35
  146.3 0.2 convolution_bitcast_fusion
  146.6 6.1 %all-to-all-done = f32[16,1,48]{2,1,0:T(1,128)S(1)} async-done(((f32[16,1,48]{2,1,0:T(1,128)}), f32[16,1,48]{2,1,0:T(1,128)S(1)}, u32[]{:S(2)}, u32[]{:S(2)}) %all-to-all-start) | async-done | bytes 3104 | tf_op jit(solution)/shard_map/all_to_all | solution.py:35
  152.7 0.0 copy-start.1
  152.8 0.2 convolution_bitcast_fusion.1
  153.0 38.2 %all-reduce = (f32[64]{0:T(128)S(1)}, f32[64]{0:T(128)S(1)}) all-reduce(f32[64]{0:T(128)S(1)} %convolution_bitcast_fusion.1, f32[64]{0:T(128)S(1)} %convolution_bitcast_fusion), channel_id=1, replica_groups=mesh['tok'=2,'vocab'=16] {'tok','vocab'}, use_global_device_ids=true, to_apply=%region_7.8 | all-reduce | flops 128 | bytes 1024 | tf_op jit(solution)/shard_map/psum | solution.py:65
  191.1 0.5 maximum_divide_fusion
  191.6 0.0 copy-done.1
  (6 shorter events, 0.1 us)
Async XLA Ops:
  7.2 94.7 %all-gather.2.cloned.1.call-start = ((), (), s32[]{:S(2)}) async-start(), calls=%async_computation.3 | async-start | bytes 6684672 | tf_op jit(solution)/shard_map/all_gather | solution.py:11
  7.9 93.9 %collective-permute-start = (bf16[2048,1024]{1,0:T(8,128)(2,1)}, bf16[2048,1024]{1,0:T(8,128)(2,1)}, u32[]{:S(2)}, u32[]{:S(2)}) collective-permute-start(bf16[2048,1024]{1,0:T(8,128)(2,1)} %param.6), channel_id=1, source_target_pairs={{0,16},{16,0},{1,17},{17,1},{2,18},{18,2},{3,19},{19,3},{4,20},{20... | collective-permute-start | bytes 12582920 | tf_op jit(solution)/shard_map/ppermute | solution.py:17
  11.0 115.6 %copy-start = (s32[768]{0:T(1024)S(1)}, s32[768]{0:T(1024)}, u32[]{:S(2)}) copy-start(s32[768]{0:T(1024)} %param.7) | copy-start | bytes 9220
  11.0 125.5 %copy-start.2 = (s32[6]{0:T(128)S(1)}, s32[6]{0:T(128)}, u32[]{:S(2)}) copy-start(s32[6]{0:T(128)} %param.9) | copy-start | bytes 76
  120.4 12.6 %all-to-all-start.1 = ((f32[16,1,48]{2,1,0:T(1,128)}), f32[16,1,48]{2,1,0:T(1,128)S(1)}, u32[]{:S(2)}, u32[]{:S(2)}) async-start(f32[16,1,48]{2,1,0:T(1,128)} %all_to_all.25), calls=%async_computation.1 | async-start | bytes 16384 | tf_op jit(solution)/shard_map/all_to_all | solution.py:32
  133.0 9.9 %all-to-all-start.2 = ((f32[16,1,48]{2,1,0:T(1,128)}), f32[16,1,48]{2,1,0:T(1,128)S(1)}, u32[]{:S(2)}, u32[]{:S(2)}) async-start(f32[16,1,48]{2,1,0:T(1,128)} %all_to_all.28), calls=%async_computation.2 | async-start | bytes 16384 | tf_op jit(solution)/shard_map/all_to_all | solution.py:38
  142.9 9.8 %all-to-all-start = ((f32[16,1,48]{2,1,0:T(1,128)}), f32[16,1,48]{2,1,0:T(1,128)S(1)}, u32[]{:S(2)}, u32[]{:S(2)}) async-start(f32[16,1,48]{2,1,0:T(1,128)} %all_to_all.22), calls=%async_computation | async-start | bytes 16384 | tf_op jit(solution)/shard_map/all_to_all | solution.py:35
  152.7 38.9 %copy-start.1 = (f32[48]{0:T(128)}, f32[48]{0:T(128)S(1)}, u32[]{:S(2)}) copy-start(f32[48]{0:T(128)S(1)} %subtract_select_fusion) | copy-start | bytes 580
Sparse Core Ops, SparseCore 0:
  10.1 67.9 all-gather.1
